TPU v7x, 32 devices: a whole 2x2x4 slice. The times are simulated.
32 devices in a mesh: gx: 4 (over z), gy: 2 (over y), gz: 4 (over x, core).
Axes of the slice: x: 2, y: 2, z: 4, core: 2. Of those that a mesh axis runs over, the one named last changes fastest.
Arguments:
- hidden_acts: bfloat16 [4, 2, 4, 256, 16384], P('gz', 'gy', 'gx'), may hold values from -6 to 6
- output_grad: bfloat16 [4, 2, 4, 256, 32], P('gz', 'gy', 'gx'), may hold values from -6 to 6
- weights: bfloat16 [4, 2, 4, 32, 16384], P('gz', 'gy', 'gx'), may hold values from -6 to 6
- momentum: bfloat16 [4, 2, 4, 32, 16384], P('gz', 'gy', 'gx'), may hold values from -48 to 48
- worker_of_slot: int32 [32], replicated, may hold values from 0 to 31, each once
- round_shift: int32 [8], replicated, may hold values from 0 to 4, as said below
Outputs:
- mixed: bfloat16 [4, 2, 4, 32, 16384], P('gx', 'gy', 'gz')
- new_momentum: bfloat16 [4, 2, 4, 32, 16384], P('gz', 'gy', 'gx')
Inputs may be any that keep to these rules, and one draw needn't show every extreme that they name: `round_shift`: each entry is below log2 of 32, so offsets are powers of two below 32; some round has offset 32 / 2 and some round offset 1.
All inputs are finite; a program needn't handle non-finite values.
Results may differ from a plain program's by a relative error of at most 0.0081.
Values may be sent and summed in bfloat16 or wider, within the bound.
A program may use at most 64 MiB of HBM per device.

v0:
```python
import jax
import jax.numpy as jnp
from jax import lax
from jax.sharding import PartitionSpec as P

ROUNDS = 8


learn_rate = 0.01
beta_keep = 0.9


def for_sending(shard):
    return jax.tree.map(lambda a: a.astype(jnp.bfloat16) if a.dtype == jnp.float32 else a, shard)


def shifted(value, axis, steps):
    count = lax.axis_size(axis)
    pairs = [(source, (source + steps) % count) for source in range(count)]
    return lax.ppermute(value, axis, pairs)


def spread(block, select, outer, workers):
    pieces = block.reshape(outer, workers // outer, block.size // workers)
    moved = lax.all_to_all(
        lax.all_to_all(pieces, "gx", split_axis=0, concat_axis=0, tiled=True),
        ("gy", "gz"),
        split_axis=1,
        concat_axis=1,
        tiled=True,
    )
    rows_all = jnp.take(moved.reshape(workers, -1), select, axis=0)
    back = lax.all_to_all(
        lax.all_to_all(
            rows_all.reshape(pieces.shape), "gx", split_axis=0, concat_axis=0, tiled=True
        ),
        ("gy", "gz"),
        split_axis=1,
        concat_axis=1,
        tiled=True,
    )
    return back.reshape(block.shape)


def from_all(value, power):
    return jax.tree.map(
        lambda part, own: part.astype(own.dtype),
        shifted(for_sending(value), ("gx", "gy", "gz"), 1 << power),
        value,
    )


def shards(hidden_acts, output_grad, weights, momentum, worker_of_slot, round_shift):
    hidden = hidden_acts.reshape(hidden_acts.shape[-2:])
    grad_out = output_grad.reshape(output_grad.shape[-2:])
    weight = weights.reshape(weights.shape[-2:])
    moment = momentum.reshape(momentum.shape[-2:])
    grad = lax.dot_general(
        grad_out, hidden, (((0,), (0,)), ((), ())), preferred_element_type=jnp.float32
    )
    velocity = beta_keep * moment.astype(jnp.float32) + grad
    new_moment = velocity.astype(jnp.bfloat16)
    stepped = (weight.astype(jnp.float32) - learn_rate * velocity).astype(jnp.bfloat16)
    count_x = lax.axis_size("gx")
    count_y = lax.axis_size("gy")
    count_z = lax.axis_size("gz")
    workers = count_x * count_y * count_z
    joined = jnp.arange(workers, dtype=jnp.int32)
    digit_x = joined // (count_y * count_z)
    digit_y = joined // count_z % count_y
    digit_z = joined % count_z
    slots = digit_x + count_x * (digit_y + count_y * digit_z)
    held = jnp.take(worker_of_slot, slots, axis=0)
    source = jnp.zeros((workers,), jnp.int32).at[held].set(joined)
    levels = workers.bit_length() - 1
    branches = []
    block = spread(stepped, source, count_x, workers)
    for level in range(levels):
        branches.append(lambda value, power=level: from_all(value, power))
    for step in range(ROUNDS):
        received = lax.switch(round_shift[step], branches, block)
        block = ((block.astype(jnp.float32) + received.astype(jnp.float32)) * 0.5).astype(
            jnp.bfloat16
        )
    return (block.reshape(weights.shape), new_moment.reshape(momentum.shape))


def solution(mesh):
    placed = (
        P("gz", "gy", "gx", None, None),
        P("gz", "gy", "gx", None, None),
        P("gz", "gy", "gx", None, None),
        P("gz", "gy", "gx", None, None),
        P(),
        P(),
    )
    return jax.shard_map(
        shards,
        mesh=mesh,
        in_specs=placed,
        out_specs=(P("gx", "gy", "gz", None, None), P("gz", "gy", "gx", None, None)),
        check_vma=False,
    )
```

profile of v0, /device:TPU:0, one launch (start us, length us, event | category | flops | bytes accessed | tf_op | source)
XLA Modules:
  0.0 371.1 jit_solution(7476020280276403211)
XLA Ops:
  0.6 0.7 copy-done
  1.4 6.6 %convert_bitcast_fusion = (bf16[1,1,1,32,16384]{4,3,2,1,0:T(8,128)(2,1)}, bf16[4,8,16384]{2,1,0:T(8,128)(2,1)S(1)}) fusion(bf16[1,1,1,32,16384]{4,3,2,1,0:T(8,128)(2,1)} %param.48, bf16[1,1,1,256,16384]{4,3,2,1,0:T(8,128)(2,1)} %param.46, bf16[1,1,1,256,32]{3,4,2,1,0:T(8,128)(2,1)S(1)} %copy-done, bf16[1,1,1,32,16384]{4,3,2,1,0:T(8,128)(2,1)} %param.49), kind=kOutput, calls=%fused_computation.20 | convolution fusion | flops 272629760 | bytes 12599296 | tf_op jit(solution)/shard_map/dot_general | solution.py:58
  7.9 31.9 %all_to_all.20 = bf16[4,8,16384]{2,1,0:T(8,128)(2,1)S(1)} all-to-all(bf16[4,8,16384]{2,1,0:T(8,128)(2,1)S(1)} %get-tuple-element.139), channel_id=1, replica_groups=mesh['gx'=4,'gy'=2,'gz'=4] {'gx'}, dimensions={0} | all-to-all | bytes 2097152 | tf_op jit(solution)/shard_map/all_to_all | solution.py:26
  39.8 1.8 copy.17
  41.6 3.7 %all-to-all-start.1 = ((bf16[4,8,16384]{2,0,1:T(4,128)(2,1)}), bf16[4,8,16384]{2,0,1:T(4,128)(2,1)S(1)}, u32[]{:S(2)}, u32[]{:S(2)}) async-start(bf16[4,8,16384]{2,0,1:T(4,128)(2,1)} %copy.17), calls=%async_computation.1 | async-start | bytes 2097152 | tf_op jit(solution)/shard_map/all_to_all | solution.py:25
  45.3 0.7 gather_fusion
  46.1 0.7 scatter_custom_fusion
  46.8 0.1 broadcast_in_dim.22
  46.9 13.8 %all-to-all-done.1 = bf16[4,8,16384]{2,0,1:T(4,128)(2,1)S(1)} async-done(((bf16[4,8,16384]{2,0,1:T(4,128)(2,1)}), bf16[4,8,16384]{2,0,1:T(4,128)(2,1)S(1)}, u32[]{:S(2)}, u32[]{:S(2)}) %all-to-all-start.1) | async-done | bytes 1048608 | tf_op jit(solution)/shard_map/all_to_all | solution.py:25
  60.7 0.6 copy.26
  61.3 1.2 gather_fusion.1
  62.5 0.2 bitcast_select_fusion
  62.7 25.7 %all_to_all.21 = bf16[4,8,16384]{2,1,0:T(8,128)(2,1)S(1)} all-to-all(bf16[4,8,16384]{2,1,0:T(8,128)(2,1)S(1)} %bitcast_select_fusion), channel_id=1, replica_groups=mesh['gx'=4,'gy'=2,'gz'=4] {'gx'}, dimensions={0} | all-to-all | bytes 2097152 | tf_op jit(solution)/shard_map/all_to_all | solution.py:34
  88.3 1.8 copy.19
  90.1 4.8 %all-to-all-start.3 = ((bf16[4,8,16384]{2,0,1:T(4,128)(2,1)}), bf16[4,8,16384]{2,0,1:T(4,128)(2,1)S(1)}, u32[]{:S(2)}, u32[]{:S(2)}) async-start(bf16[4,8,16384]{2,0,1:T(4,128)(2,1)} %copy.19), calls=%async_computation.3 | async-start | bytes 2097152 | tf_op jit(solution)/shard_map/all_to_all | solution.py:33
  94.9 0.7 fusion.14
  100.6 9.7 %all-to-all-done.3 = bf16[4,8,16384]{2,0,1:T(4,128)(2,1)S(1)} async-done(((bf16[4,8,16384]{2,0,1:T(4,128)(2,1)}), bf16[4,8,16384]{2,0,1:T(4,128)(2,1)S(1)}, u32[]{:S(2)}, u32[]{:S(2)}) %all-to-all-start.3) | async-done | bytes 1048608 | tf_op jit(solution)/shard_map/all_to_all | solution.py:33
  110.3 0.6 copy.25
  110.8 18.0 %conditional.32 = (bf16[32,16384]{1,0:T(8,128)(2,1)}) conditional(s32[]{:T(128)} %bitcast.11, bf16[32,16384]{1,0:T(8,128)(2,1)S(1)} %bitcast.51, bf16[32,16384]{1,0:T(8,128)(2,1)S(1)} %bitcast.52, bf16[32,16384]{1,0:T(8,128)(2,1)S(1)} %bitcast.53, bf16[32,16384]{1,0:T(8,128)(2,1)S(1)} %bitcast.54, ...), branch_computations={%region_1.2_spmd, %region_2.3_spmd, %region_3.4_spmd, %region_4.5_... | conditional | bytes 4194352
  110.9 0.1 collective-permute-start
  110.9 17.9 %collective-permute-done = bf16[32,16384]{1,0:T(8,128)(2,1)} collective-permute-done((bf16[32,16384]{1,0:T(8,128)(2,1)S(1)}, bf16[32,16384]{1,0:T(8,128)(2,1)}, u32[]{:S(2)}, u32[]{:S(2)}) %collective-permute-start) | collective-permute-done | bytes 1048608 | tf_op jit(solution)/shard_map/cond/branch_0_fun/ppermute | solution.py:20
  128.8 1.9 multiply_convert_fusion.7
  130.7 19.4 %conditional.33 = (bf16[32,16384]{1,0:T(8,128)(2,1)}) conditional(s32[]{:T(128)} %bitcast.12, bf16[32,16384]{1,0:T(8,128)(2,1)S(1)} %multiply_convert_fusion.7, bf16[32,16384]{1,0:T(8,128)(2,1)S(1)} %multiply_convert_fusion.7, bf16[32,16384]{1,0:T(8,128)(2,1)S(1)} %multiply_convert_fusion.7, ...), branch_computations={%region_6.7_spmd, %region_7.8_spmd, %region_8.9_spmd, %region_9.10... | conditional | bytes 4194352
  130.8 19.3 %collective-permute-done.5 = bf16[32,16384]{1,0:T(8,128)(2,1)} collective-permute-done((bf16[32,16384]{1,0:T(8,128)(2,1)S(1)}, bf16[32,16384]{1,0:T(8,128)(2,1)}, u32[]{:S(2)}, u32[]{:S(2)}) %collective-permute-start.5) | collective-permute-done | bytes 1048608 | tf_op jit(solution)/shard_map/cond/branch_0_fun/ppermute | solution.py:20
  150.1 1.5 multiply_convert_fusion.6
  151.7 37.7 %conditional.34 = (bf16[32,16384]{1,0:T(8,128)(2,1)}) conditional(s32[]{:T(128)} %bitcast.13, bf16[32,16384]{1,0:T(8,128)(2,1)S(1)} %multiply_convert_fusion.6, bf16[32,16384]{1,0:T(8,128)(2,1)S(1)} %multiply_convert_fusion.6, bf16[32,16384]{1,0:T(8,128)(2,1)S(1)} %multiply_convert_fusion.6, ...), branch_computations={%region_11.12_spmd, %region_12.13_spmd, %region_13.14_spmd, %regio... | conditional | bytes 4194352
  151.7 0.1 collective-permute-start.14
  151.8 37.6 %collective-permute-done.14 = bf16[32,16384]{1,0:T(8,128)(2,1)} collective-permute-done((bf16[32,16384]{1,0:T(8,128)(2,1)S(1)}, bf16[32,16384]{1,0:T(8,128)(2,1)}, u32[]{:S(2)}, u32[]{:S(2)}) %collective-permute-start.14) | collective-permute-done | bytes 1048608 | tf_op jit(solution)/shard_map/cond/branch_4_fun/ppermute | solution.py:20
  189.4 1.5 multiply_convert_fusion.5
  190.9 27.1 %conditional.35 = (bf16[32,16384]{1,0:T(8,128)(2,1)}) conditional(s32[]{:T(128)} %bitcast.14, bf16[32,16384]{1,0:T(8,128)(2,1)S(1)} %multiply_convert_fusion.5, bf16[32,16384]{1,0:T(8,128)(2,1)S(1)} %multiply_convert_fusion.5, bf16[32,16384]{1,0:T(8,128)(2,1)S(1)} %multiply_convert_fusion.5, ...), branch_computations={%region_16.17_spmd, %region_17.18_spmd, %region_18.19_spmd, %regio... | conditional | bytes 4194352
  190.9 0.1 collective-permute-start.18
  191.0 27.0 %collective-permute-done.18 = bf16[32,16384]{1,0:T(8,128)(2,1)} collective-permute-done((bf16[32,16384]{1,0:T(8,128)(2,1)S(1)}, bf16[32,16384]{1,0:T(8,128)(2,1)}, u32[]{:S(2)}, u32[]{:S(2)}) %collective-permute-start.18) | collective-permute-done | bytes 1048608 | tf_op jit(solution)/shard_map/cond/branch_3_fun/ppermute | solution.py:20
  218.0 1.5 multiply_convert_fusion.4
  219.5 27.1 %conditional.36 = (bf16[32,16384]{1,0:T(8,128)(2,1)}) conditional(s32[]{:T(128)} %bitcast.15, bf16[32,16384]{1,0:T(8,128)(2,1)S(1)} %multiply_convert_fusion.4, bf16[32,16384]{1,0:T(8,128)(2,1)S(1)} %multiply_convert_fusion.4, bf16[32,16384]{1,0:T(8,128)(2,1)S(1)} %multiply_convert_fusion.4, ...), branch_computations={%region_21.22_spmd, %region_22.23_spmd, %region_23.24_spmd, %regio... | conditional | bytes 4194352
  219.5 0.7 collective-permute-start.22
  220.2 26.4 %collective-permute-done.22 = bf16[32,16384]{1,0:T(8,128)(2,1)} collective-permute-done((bf16[32,16384]{1,0:T(8,128)(2,1)S(1)}, bf16[32,16384]{1,0:T(8,128)(2,1)}, u32[]{:S(2)}, u32[]{:S(2)}) %collective-permute-start.22) | collective-permute-done | bytes 1048608 | tf_op jit(solution)/shard_map/cond/branch_2_fun/ppermute | solution.py:20
  246.6 1.5 multiply_convert_fusion.3
  248.2 44.3 %conditional.37 = (bf16[32,16384]{1,0:T(8,128)(2,1)}) conditional(s32[]{:T(128)} %bitcast.16, bf16[32,16384]{1,0:T(8,128)(2,1)S(1)} %multiply_convert_fusion.3, bf16[32,16384]{1,0:T(8,128)(2,1)S(1)} %multiply_convert_fusion.3, bf16[32,16384]{1,0:T(8,128)(2,1)S(1)} %multiply_convert_fusion.3, ...), branch_computations={%region_26.27_spmd, %region_27.28_spmd, %region_28.29_spmd, %regio... | conditional | bytes 4194352
  248.2 0.1 collective-permute-start.29
  248.3 44.2 %collective-permute-done.29 = bf16[32,16384]{1,0:T(8,128)(2,1)} collective-permute-done((bf16[32,16384]{1,0:T(8,128)(2,1)S(1)}, bf16[32,16384]{1,0:T(8,128)(2,1)}, u32[]{:S(2)}, u32[]{:S(2)}) %collective-permute-start.29) | collective-permute-done | bytes 1048608 | tf_op jit(solution)/shard_map/cond/branch_4_fun/ppermute | solution.py:20
  292.5 1.5 multiply_convert_fusion.2
  294.0 27.1 %conditional.38 = (bf16[32,16384]{1,0:T(8,128)(2,1)}) conditional(s32[]{:T(128)} %bitcast.17, bf16[32,16384]{1,0:T(8,128)(2,1)S(1)} %multiply_convert_fusion.2, bf16[32,16384]{1,0:T(8,128)(2,1)S(1)} %multiply_convert_fusion.2, bf16[32,16384]{1,0:T(8,128)(2,1)S(1)} %multiply_convert_fusion.2, ...), branch_computations={%region_31.32_spmd, %region_32.33_spmd, %region_33.34_spmd, %regio... | conditional | bytes 4194352
  294.1 27.0 %collective-permute-done.33 = bf16[32,16384]{1,0:T(8,128)(2,1)} collective-permute-done((bf16[32,16384]{1,0:T(8,128)(2,1)S(1)}, bf16[32,16384]{1,0:T(8,128)(2,1)}, u32[]{:S(2)}, u32[]{:S(2)}) %collective-permute-start.33) | collective-permute-done | bytes 1048608 | tf_op jit(solution)/shard_map/cond/branch_3_fun/ppermute | solution.py:20
  321.1 1.5 multiply_convert_fusion.1
  322.6 46.0 %conditional.39 = (bf16[32,16384]{1,0:T(8,128)(2,1)}) conditional(s32[]{:T(128)} %bitcast.18, bf16[32,16384]{1,0:T(8,128)(2,1)S(1)} %multiply_convert_fusion.1, bf16[32,16384]{1,0:T(8,128)(2,1)S(1)} %multiply_convert_fusion.1, bf16[32,16384]{1,0:T(8,128)(2,1)S(1)} %multiply_convert_fusion.1, ...), branch_computations={%region_36.37_spmd, %region_37.38_spmd, %region_38.39_spmd, %regio... | conditional | bytes 4194352
  322.7 0.1 collective-permute-start.39
  322.7 45.9 %collective-permute-done.39 = bf16[32,16384]{1,0:T(8,128)(2,1)} collective-permute-done((bf16[32,16384]{1,0:T(8,128)(2,1)S(1)}, bf16[32,16384]{1,0:T(8,128)(2,1)}, u32[]{:S(2)}, u32[]{:S(2)}) %collective-permute-start.39) | collective-permute-done | bytes 1048608 | tf_op jit(solution)/shard_map/cond/branch_4_fun/ppermute | solution.py:20
  368.6 2.5 fusion.2
  (14 shorter events, 0.2 us)
Async XLA Ops:
  0.6 0.7 copy-start
  39.8 5.5 %copy-start.1 = (s32[32]{0:T(128)S(1)}, s32[32]{0:T(128)}, u32[]{:S(2)}) copy-start(s32[32]{0:T(128)} %param.50) | copy-start | bytes 388
  41.6 19.1 %all-to-all-start.1 = ((bf16[4,8,16384]{2,0,1:T(4,128)(2,1)}), bf16[4,8,16384]{2,0,1:T(4,128)(2,1)S(1)}, u32[]{:S(2)}, u32[]{:S(2)}) async-start(bf16[4,8,16384]{2,0,1:T(4,128)(2,1)} %copy.17), calls=%async_computation.1 | async-start | bytes 2097152 | tf_op jit(solution)/shard_map/all_to_all | solution.py:25
  88.3 6.6 %copy-start.2 = (s32[8]{0:T(128)S(1)}, s32[8]{0:T(128)}, u32[]{:S(2)}) copy-start(s32[8]{0:T(128)} %param.51) | copy-start | bytes 100
  90.1 20.1 %all-to-all-start.3 = ((bf16[4,8,16384]{2,0,1:T(4,128)(2,1)}), bf16[4,8,16384]{2,0,1:T(4,128)(2,1)S(1)}, u32[]{:S(2)}, u32[]{:S(2)}) async-start(bf16[4,8,16384]{2,0,1:T(4,128)(2,1)} %copy.19), calls=%async_computation.3 | async-start | bytes 2097152 | tf_op jit(solution)/shard_map/all_to_all | solution.py:33
  110.9 18.0 %collective-permute-start = (bf16[32,16384]{1,0:T(8,128)(2,1)S(1)}, bf16[32,16384]{1,0:T(8,128)(2,1)}, u32[]{:S(2)}, u32[]{:S(2)}) collective-permute-start(bf16[32,16384]{1,0:T(8,128)(2,1)S(1)} %param), channel_id=1, source_target_pairs={{0,1},{1,2},{2,3},{3,4},{4,5},{5,6},{6,7},{7,8},{8,9},{9,10},{10,1... | collective-permute-start | bytes 3145736 | tf_op jit(solution)/shard_map/cond/branch_0_fun/ppermute | solution.py:20
  130.7 19.4 %collective-permute-start.5 = (bf16[32,16384]{1,0:T(8,128)(2,1)S(1)}, bf16[32,16384]{1,0:T(8,128)(2,1)}, u32[]{:S(2)}, u32[]{:S(2)}) collective-permute-start(bf16[32,16384]{1,0:T(8,128)(2,1)S(1)} %param.5), channel_id=1, source_target_pairs={{0,1},{1,2},{2,3},{3,4},{4,5},{5,6},{6,7},{7,8},{8,9},{9,10},{10,1... | collective-permute-start | bytes 3145736 | tf_op jit(solution)/shard_map/cond/branch_0_fun/ppermute | solution.py:20
  151.7 37.7 %collective-permute-start.14 = (bf16[32,16384]{1,0:T(8,128)(2,1)S(1)}, bf16[32,16384]{1,0:T(8,128)(2,1)}, u32[]{:S(2)}, u32[]{:S(2)}) collective-permute-start(bf16[32,16384]{1,0:T(8,128)(2,1)S(1)} %param.14), channel_id=1, source_target_pairs={{0,16},{1,17},{2,18},{3,19},{4,20},{5,21},{6,22},{7,23},{8,24},{9,... | collective-permute-start | bytes 3145736 | tf_op jit(solution)/shard_map/cond/branch_4_fun/ppermute | solution.py:20
  190.9 27.0 %collective-permute-start.18 = (bf16[32,16384]{1,0:T(8,128)(2,1)S(1)}, bf16[32,16384]{1,0:T(8,128)(2,1)}, u32[]{:S(2)}, u32[]{:S(2)}) collective-permute-start(bf16[32,16384]{1,0:T(8,128)(2,1)S(1)} %param.18), channel_id=1, source_target_pairs={{0,8},{1,9},{2,10},{3,11},{4,12},{5,13},{6,14},{7,15},{8,16},{9,17... | collective-permute-start | bytes 3145736 | tf_op jit(solution)/shard_map/cond/branch_3_fun/ppermute | solution.py:20
  219.5 27.1 %collective-permute-start.22 = (bf16[32,16384]{1,0:T(8,128)(2,1)S(1)}, bf16[32,16384]{1,0:T(8,128)(2,1)}, u32[]{:S(2)}, u32[]{:S(2)}) collective-permute-start(bf16[32,16384]{1,0:T(8,128)(2,1)S(1)} %param.22), channel_id=1, source_target_pairs={{0,4},{1,5},{2,6},{3,7},{4,8},{5,9},{6,10},{7,11},{8,12},{9,13},{1... | collective-permute-start | bytes 3145736 | tf_op jit(solution)/shard_map/cond/branch_2_fun/ppermute | solution.py:20
  248.2 44.3 %collective-permute-start.29 = (bf16[32,16384]{1,0:T(8,128)(2,1)S(1)}, bf16[32,16384]{1,0:T(8,128)(2,1)}, u32[]{:S(2)}, u32[]{:S(2)}) collective-permute-start(bf16[32,16384]{1,0:T(8,128)(2,1)S(1)} %param.29), channel_id=1, source_target_pairs={{0,16},{1,17},{2,18},{3,19},{4,20},{5,21},{6,22},{7,23},{8,24},{9,... | collective-permute-start | bytes 3145736 | tf_op jit(solution)/shard_map/cond/branch_4_fun/ppermute | solution.py:20
  294.1 27.0 %collective-permute-start.33 = (bf16[32,16384]{1,0:T(8,128)(2,1)S(1)}, bf16[32,16384]{1,0:T(8,128)(2,1)}, u32[]{:S(2)}, u32[]{:S(2)}) collective-permute-start(bf16[32,16384]{1,0:T(8,128)(2,1)S(1)} %param.33), channel_id=1, source_target_pairs={{0,8},{1,9},{2,10},{3,11},{4,12},{5,13},{6,14},{7,15},{8,16},{9,17... | collective-permute-start | bytes 3145736 | tf_op jit(solution)/shard_map/cond/branch_3_fun/ppermute | solution.py:20
  322.7 46.0 %collective-permute-start.39 = (bf16[32,16384]{1,0:T(8,128)(2,1)S(1)}, bf16[32,16384]{1,0:T(8,128)(2,1)}, u32[]{:S(2)}, u32[]{:S(2)}) collective-permute-start(bf16[32,16384]{1,0:T(8,128)(2,1)S(1)} %param.39), channel_id=1, source_target_pairs={{0,16},{1,17},{2,18},{3,19},{4,20},{5,21},{6,22},{7,23},{8,24},{9,... | collective-permute-start | bytes 3145736 | tf_op jit(solution)/shard_map/cond/branch_4_fun/ppermute | solution.py:20
where the time goes:
time: 370 us; the launch traced here: 371 us
  waiting for transfers between devices  269 us (73%)
  blocking collectives  57.5 us (16%)
  other arithmetic  13.8 us (4%)
  starting transfers between devices  9.65 us (3%)
  local copies, waits for them, and re-layouts  8.78 us (2%)
  matrix products  6.59 us (2%)
  between operations  5.74 us (2%)
    ppermute x8, waiting for transfers between devices, shifted(): return lax.ppermute(value, axis, pairs)  245 us
    all_to_all x1, blocking collectives, spread(): lax.all_to_all(pieces, 'gx', split_axis=0, concat_axis=0, tiled=True)  31.9 us
    all_to_all x1, blocking collectives, spread(): lax.all_to_all(rows_all.reshape(pieces.shape), 'gx', split_axis=0, concat...  25.7 us
    all_to_all x1, waiting for transfers between devices, spread(): lax.all_to_all(lax.all_to_all(pieces, 'gx', split_axis=0, concat_axis=0,...  13.8 us
    convert_element_type x7, other arithmetic, shards(): ((block.astype(jnp.float32) + received.astype(jnp.float32)) * 0.5).astype...  11.1 us
    all_to_all x1, waiting for transfers between devices, spread(): lax.all_to_all(lax.all_to_all(rows_all.reshape(pieces.shape), 'gx', split...  9.69 us
  transfers between devices with their start and end apart: 10, of which 10 were waited for; matrix products, arithmetic and copies ran while one was open for 1% of the time, Pallas kernels for 0%

commit v1 on v0

v1 whole, which is shorter than its diff:
```python
import jax
import jax.numpy as jnp
from jax import lax
from jax.sharding import PartitionSpec as P

learn_rate = 0.01
beta_keep = 0.9
AXES = ("gx", "gy", "gz")


def mixing(held, round_shift, workers):
    rows = jnp.arange(workers, dtype=jnp.int32)
    share = (rows == 0).astype(jnp.float32)
    for step in range(round_shift.shape[0]):
        back = (rows - jnp.left_shift(1, round_shift[step])) % workers
        hit = (back[:, None] == rows[None, :]).astype(jnp.float32)
        share = (share + jnp.sum(hit * share[None, :], axis=1)) * 0.5
    gap = (rows[:, None] - held[None, :]) % workers
    return jnp.sum((gap[:, :, None] == rows) * share, axis=2).astype(jnp.bfloat16)


def shards(hidden_acts, output_grad, weights, momentum, worker_of_slot, round_shift):
    hidden = hidden_acts.reshape(hidden_acts.shape[-2:])
    grad_out = output_grad.reshape(output_grad.shape[-2:])
    weight = weights.reshape(weights.shape[-2:])
    moment = momentum.reshape(momentum.shape[-2:])
    grad = lax.dot_general(
        grad_out, hidden, (((0,), (0,)), ((), ())), preferred_element_type=jnp.float32
    )
    velocity = beta_keep * moment.astype(jnp.float32) + grad
    new_moment = velocity.astype(jnp.bfloat16)
    stepped = (weight.astype(jnp.float32) - learn_rate * velocity).astype(jnp.bfloat16)
    count_x = lax.axis_size("gx")
    count_y = lax.axis_size("gy")
    count_z = lax.axis_size("gz")
    workers = count_x * count_y * count_z
    held = worker_of_slot.reshape(count_z, count_y, count_x).transpose(2, 1, 0).reshape(-1)
    matrix = mixing(held, round_shift, workers)
    pieces = stepped.reshape(workers, stepped.size // workers)
    got = lax.all_to_all(pieces, AXES, split_axis=0, concat_axis=0, tiled=True)
    mixed = lax.dot_general(
        matrix, got, (((1,), (0,)), ((), ())), preferred_element_type=jnp.float32
    ).astype(jnp.bfloat16)
    block = lax.all_to_all(mixed, AXES, split_axis=0, concat_axis=0, tiled=True)
    return (block.reshape(weights.shape), new_moment.reshape(momentum.shape))


def solution(mesh):
    placed = (
        P("gz", "gy", "gx", None, None),
        P("gz", "gy", "gx", None, None),
        P("gz", "gy", "gx", None, None),
        P("gz", "gy", "gx", None, None),
        P(),
        P(),
    )
    return jax.shard_map(
        shards,
        mesh=mesh,
        in_specs=placed,
        out_specs=(P("gx", "gy", "gz", None, None), P("gz", "gy", "gx", None, None)),
        check_vma=False,
    )
```

time: 370 us -> 83.2 us (0.22)
  waiting for transfers between devices: 269 us -> 18.2 us
  blocking collectives: 57.5 us -> 29.6 us
  other arithmetic: 13.8 us -> 4.95 us
    ppermute x8 -> x0, waiting for transfers between devices: 245 us -> none  [shifted(): return lax.ppermute(value, axis, pairs)]
    all_to_all x2 -> x1, blocking collectives: 57.5 us -> 29.6 us  [shards(): block = lax.all_to_all(mixed, AXES, split_axis=0, concat_axis=0, tiled=True)]
    convert_element_type x7 -> x1, other arithmetic: 11.1 us -> 0.01 us  [mixing(): share = (rows == 0).astype(jnp.float32)]
    unnamed x6 -> x11, local copies, waits for them, and re-layouts: 0.72 us -> 7.31 us
    all_to_all x2 -> x1, waiting for transfers between devices: 23.5 us -> 18.2 us  [shards(): got = lax.all_to_all(pieces, AXES, split_axis=0, concat_axis=0, tiled=True)]
    all_to_all x4 -> x1, local copies, waits for them, and re-layouts: 4.72 us -> 0.59 us  [shards(): got = lax.all_to_all(pieces, AXES, split_axis=0, concat_axis=0, tiled=True)]
    all_to_all x2 -> x1, starting transfers between devices: 8.49 us -> 7.32 us  [shards(): got = lax.all_to_all(pieces, AXES, split_axis=0, concat_axis=0, tiled=True)]
  transfers between devices with their start and end apart: 10 -> 1, of which waited for: 10 -> 1; matrix products, arithmetic and copies ran while one was open for 1% -> 4% of each run, Pallas kernels for 0% -> 0%
where the time goes in v1:
time: 83.2 us; the launch traced here: 82.8 us
  blocking collectives  29.6 us (36%)
  waiting for transfers between devices  18.2 us (22%)
  local copies, waits for them, and re-layouts  8.86 us (11%)
  matrix products  8.11 us (10%)
  starting transfers between devices  7.32 us (9%)
  between operations  5.81 us (7%)
  other arithmetic  4.95 us (6%)
    all_to_all x1, blocking collectives, shards(): block = lax.all_to_all(mixed, AXES, split_axis=0, concat_axis=0, tiled=True)  29.6 us
    all_to_all x1, waiting for transfers between devices, shards(): got = lax.all_to_all(pieces, AXES, split_axis=0, concat_axis=0, tiled=True)  18.2 us
    all_to_all x1, starting transfers between devices, shards(): got = lax.all_to_all(pieces, AXES, split_axis=0, concat_axis=0, tiled=True)  7.32 us
    unnamed x11, local copies, waits for them, and re-layouts  7.31 us
    dot_general x1, matrix products, shards(): lax.dot_general(grad_out, hidden, (((0,), (0,)), ((), ())), preferred_ele...  6.59 us
  transfers between devices with their start and end apart: 1, of which 1 were waited for; matrix products, arithmetic and copies ran while one was open for 4% of the time, Pallas kernels for 0%

profile of v1, /device:TPU:0, one launch (start us, length us, event | category | flops | bytes accessed | tf_op | source)
XLA Modules:
  0.0 82.8 jit_solution(15236451091352223493)
XLA Ops:
  0.6 0.0 copy-start
  0.6 0.7 copy-done
  1.4 6.6 %convert_bitcast_fusion = (bf16[1,1,1,32,16384]{4,3,2,1,0:T(8,128)(2,1)}, bf16[32,1,16384]{2,0,1:T(8,128)(2,1)S(1)}) fusion(bf16[1,1,1,32,16384]{4,3,2,1,0:T(8,128)(2,1)} %param.8, bf16[1,1,1,256,16384]{4,3,2,1,0:T(8,128)(2,1)} %param.6, bf16[1,1,1,256,32]{3,4,2,1,0:T(8,128)(2,1)S(1)} %copy-done, bf16[1,1,1,32,16384]{4,3,2,1,0:T(8,128)(2,1)} %param.9), kind=kOutput, calls=%fused_computation.10 | convolution fusion | flops 272629760 | bytes 12599296 | tf_op jit(solution)/shard_map/dot_general | solution.py:27
  7.9 0.6 broadcast.437
  8.5 1.5 %reduce = bf16[32,16384]{1,0:T(8,128)(2,1)S(1)} reduce(bf16[32,1,16384]{2,0,1:T(8,128)(2,1)S(1)} %get-tuple-element.3, bf16[]{:T(256)} %broadcast.437), dimensions={1}, to_apply=%copy.16.reduce_sub_computation | reduce | bytes 2097154 | tf_op jit(solution)/shard_map/all_to_all | solution.py:40
  10.0 0.0 copy-start.2
  10.0 0.0 copy-start.1
  10.0 1.6 %reshape.331 = bf16[32,2,8192]{2,1,0:T(2,128)(2,1)} reshape(bf16[32,16384]{1,0:T(8,128)(2,1)S(1)} %reduce) | data formatting | bytes 2097152
  11.6 7.3 %all-to-all-start = ((bf16[32,2,8192]{2,1,0:T(2,128)(2,1)}), bf16[32,2,8192]{2,1,0:T(2,128)(2,1)S(1)}, u32[]{:S(2)}, u32[]{:S(2)}) async-start(bf16[32,2,8192]{2,1,0:T(2,128)(2,1)} %reshape.331), calls=%async_computation | async-start | bytes 2097152 | tf_op jit(solution)/shard_map/all_to_all | solution.py:40
  19.0 0.0 copy-done.2
  19.0 0.1 reshape.325
  19.1 0.1 copy.15
  19.2 0.1 sub.103
  19.3 0.0 copy-done.1
  19.3 0.7 fusion.20
  25.0 0.2 select_reduce_fusion.8
  25.2 0.2 select_reduce_fusion.7
  25.4 0.2 select_reduce_fusion.6
  25.6 0.2 select_reduce_fusion.5
  25.8 0.2 select_reduce_fusion.4
  26.0 0.2 select_reduce_fusion.3
  26.2 0.2 select_reduce_fusion.2
  26.4 0.2 select_reduce_fusion.1
  26.6 0.4 select_reduce_fusion
  27.0 18.2 %all-to-all-done = bf16[32,2,8192]{2,1,0:T(2,128)(2,1)S(1)} async-done(((bf16[32,2,8192]{2,1,0:T(2,128)(2,1)}), bf16[32,2,8192]{2,1,0:T(2,128)(2,1)S(1)}, u32[]{:S(2)}, u32[]{:S(2)}) %all-to-all-start) | async-done | bytes 1048608 | tf_op jit(solution)/shard_map/all_to_all | solution.py:40
  45.2 1.0 %reshape.332 = bf16[32,1,16384]{2,1,0:T(2,128)(2,1)S(1)} reshape(bf16[32,2,8192]{2,1,0:T(2,128)(2,1)S(1)} %all-to-all-done) | data formatting | bytes 2097152
  46.2 1.5 %fusion = bf16[32,1,16384]{2,0,1:T(8,128)(2,1)S(1)} fusion(bf16[32,1,16384]{2,1,0:T(2,128)(2,1)S(1)} %reshape.332, bf16[32,32]{1,0:T(8,128)(2,1)S(1)} %select_reduce_fusion), kind=kOutput, calls=%fused_computation.2 | convolution fusion | flops 34078720 | bytes 2099200 | tf_op jit(solution)/shard_map/dot_general | solution.py:41
  47.7 1.5 %reduce.1 = bf16[32,16384]{1,0:T(8,128)(2,1)S(1)} reduce(bf16[32,1,16384]{2,0,1:T(8,128)(2,1)S(1)} %fusion, bf16[]{:T(256)} %broadcast.437), dimensions={1}, to_apply=%copy.17.reduce_sub_computation | reduce | bytes 2097154 | tf_op jit(solution)/shard_map/all_to_all | solution.py:44
  49.2 0.8 reshape.333
  50.0 29.6 %all_to_all.21 = bf16[32,2,8192]{2,1,0:T(2,128)(2,1)S(1)} all-to-all(bf16[32,2,8192]{2,1,0:T(2,128)(2,1)S(1)} %reshape.333), channel_id=1, replica_groups=mesh['gx'=4,'gy'=2,'gz'=4] {'gx','gy','gz'}, dimensions={0} | all-to-all | bytes 2097152 | tf_op jit(solution)/shard_map/all_to_all | solution.py:44
  79.7 1.0 %reshape.334 = bf16[32,1,16384]{2,1,0:T(2,128)(2,1)S(1)} reshape(bf16[32,2,8192]{2,1,0:T(2,128)(2,1)S(1)} %all_to_all.21) | data formatting | bytes 2097152
  80.7 2.1 %copy.25 = bf16[32,1,16384]{2,0,1:T(8,128)(2,1)} copy(bf16[32,1,16384]{2,1,0:T(2,128)(2,1)S(1)} %reshape.334) | data formatting | bytes 2097152
  (18 shorter events, 0.2 us)
Async XLA Ops:
  0.6 0.7 copy-start
  10.0 9.0 %copy-start.2 = (s32[32]{0:T(128)S(1)}, s32[32]{0:T(128)}, u32[]{:S(2)}) copy-start(s32[32]{0:T(128)} %param.10) | copy-start | bytes 388
  10.0 9.2 %copy-start.1 = (s32[8]{0:T(128)S(1)}, s32[8]{0:T(128)}, u32[]{:S(2)}) copy-start(s32[8]{0:T(128)} %param.11) | copy-start | bytes 100
  11.6 33.5 %all-to-all-start = ((bf16[32,2,8192]{2,1,0:T(2,128)(2,1)}), bf16[32,2,8192]{2,1,0:T(2,128)(2,1)S(1)}, u32[]{:S(2)}, u32[]{:S(2)}) async-start(bf16[32,2,8192]{2,1,0:T(2,128)(2,1)} %reshape.331), calls=%async_computation | async-start | bytes 2097152 | tf_op jit(solution)/shard_map/all_to_all | solution.py:40

commit v2 on v1

v2 whole, which is shorter than its diff:
```python
import functools

import jax
import jax.numpy as jnp
from jax import lax
from jax.experimental import pallas as pl
from jax.experimental.pallas import tpu as pltpu
from jax.sharding import PartitionSpec as P

learn_rate = 0.01
beta_keep = 0.9
TILE = 16
MESH = pl.DeviceIdType.MESH


def iota(shape, axis):
    return lax.broadcasted_iota(jnp.int32, shape, axis)


def ones_where(mask):
    return jnp.where(mask, 1.0, 0.0).astype(jnp.bfloat16)


def exact_dot(a, b):
    return jnp.dot(a, b, preferred_element_type=jnp.float32)


def kernel(
    sizes,
    hidden_hbm,
    grad_ref,
    weight_hbm,
    moment_hbm,
    held_ref,
    shift_ref,
    out_ref,
    new_moment_ref,
    hidden,
    weight,
    moment,
    stage,
    recv,
    mixed,
    spread,
    hidden_sem,
    local_sem,
    send_sem,
    recv_sem,
    back_send_sem,
    back_recv_sem,
):
    size_x, size_y, size_z = sizes
    workers = size_x * size_y * size_z
    columns, _, width = hidden.shape
    parts = out_ref.shape[0] // TILE
    chunks = recv.shape[0]
    rounds = shift_ref.shape[0]
    my_x, my_y, my_z = lax.axis_index("gx"), lax.axis_index("gy"), lax.axis_index("gz")
    me = (my_x * size_y + my_y) * size_z + my_z
    slot = my_x + size_x * (my_y + size_y * my_z)
    half_x = size_x // 2

    def target(step):
        per = workers // 2
        far = 1 - lax.div(step, per)
        rest = lax.rem(step, per)
        side = lax.div(my_x, half_x)
        other = far + side - 2 * far * side
        to_x = other * half_x + lax.rem(my_x + lax.div(rest, size_y * size_z), half_x)
        to_y = lax.rem(my_y + lax.rem(lax.div(rest, size_z), size_y), size_y)
        to_z = lax.rem(my_z + lax.rem(rest, size_z), size_z)
        return (to_x * size_y + to_y) * size_z + to_z

    def coordinates(device):
        return {
            "gx": lax.div(device, size_y * size_z),
            "gy": lax.rem(lax.div(device, size_z), size_y),
            "gz": lax.rem(device, size_z),
        }

    def column(step):
        return target(step) if columns == workers else lax.rem(me + step, columns)

    def load(step):
        place = column(step)
        return pltpu.make_async_copy(
            hidden_hbm.at[:, pl.ds(pl.multiple_of(place * width, 128), width)],
            hidden.at[place],
            hidden_sem.at[step],
        )

    weight_copy = pltpu.make_async_copy(weight_hbm, weight, local_sem.at[0])
    moment_copy = pltpu.make_async_copy(moment_hbm, moment, local_sem.at[1])
    weight_copy.start()
    moment_copy.start()
    lax.fori_loop(0, columns, lambda step, c: (load(step).start(), c)[1], 0)

    barrier = pltpu.get_barrier_semaphore()

    def greet(step, carry):
        device = target(step)

        @pl.when(device != me)
        def _():
            pl.semaphore_signal(
                barrier, inc=1, device_id=coordinates(device), device_id_type=MESH
            )

        return carry

    lax.fori_loop(0, workers, greet, 0)
    grad_rows = jnp.transpose(grad_ref[...].astype(jnp.float32)).astype(jnp.bfloat16)
    weight_copy.wait()
    moment_copy.wait()
    pl.semaphore_wait(barrier, workers - 1)

    def place_of(part, where):
        block = part * columns
        return block // workers, block % workers + where

    def send(part, where):
        chunk, device = place_of(part, where)

        @pl.when(device != me)
        def _():
            pltpu.make_async_remote_copy(
                src_ref=stage.at[part, where],
                dst_ref=recv.at[chunk, slot],
                send_sem=send_sem.at[chunk],
                recv_sem=recv_sem.at[chunk],
                device_id=coordinates(device),
                device_id_type=MESH,
            ).start()

    early = [part for part in range(parts) if place_of(part, 0)[0] == 0]
    late = [part for part in range(parts) if place_of(part, 0)[0] > 0]

    def compute(step, carry):
        where = column(step)
        load(step).wait()
        span = pl.ds(pl.multiple_of(where * width, 128), width)
        grad = exact_dot(grad_rows, hidden[where])
        velocity = beta_keep * moment[:, span].astype(jnp.float32) + grad
        new_moment_ref[:, span] = velocity.astype(jnp.bfloat16)
        stepped = (weight[:, span].astype(jnp.float32) - learn_rate * velocity).astype(
            jnp.bfloat16
        )
        for part in range(parts):
            piece = stepped[part * TILE : (part + 1) * TILE]
            stage[part, where] = piece
            chunk, device = place_of(part, where)

            @pl.when(device == me)
            def _():
                recv[chunk, slot] = piece

        @pl.when(step > 0)
        def _():
            for part in early:
                send(part, column(step - 1))

        return carry

    lax.fori_loop(0, columns, compute, 0)
    for part in early:
        send(part, column(jnp.int32(columns - 1)))
    for part in late:
        lax.fori_loop(0, columns, lambda step, c: (send(part, column(step)), c)[1], 0)

    square = (workers, workers)
    gap = lax.rem(iota(square, 0) - iota(square, 1) + workers, workers)
    level = jnp.full(square, -1, jnp.int32)
    for power in range(workers.bit_length() - 1):
        level = jnp.where(gap == 1 << power, power, level)
    table = ones_where(held_ref[...] == iota(square, 0))
    for step in range(rounds):
        turn = ones_where((gap == 0) | (level == shift_ref[step]))
        table = exact_dot(turn, table).astype(jnp.bfloat16)
    distinct = workers // 2
    table = (table[:distinct].astype(jnp.float32) * 0.5**rounds).astype(jnp.bfloat16)
    wide = (workers, workers * TILE)
    table = exact_dot(table, ones_where(iota(wide, 1) // TILE == iota(wide, 0))).astype(
        jnp.bfloat16
    )
    height = min(256, distinct * TILE)

    def fill(step, carry):
        tall = (height, distinct)
        pick = ones_where((iota(tall, 0) + step * height) // TILE == iota(tall, 1))
        full = (height, workers * TILE)
        same = iota(full, 0) % TILE == iota(full, 1) % TILE
        spread[pl.ds(pl.multiple_of(step * height, height), height), :] = jnp.where(
            same, exact_dot(pick, table), 0.0
        ).astype(jnp.bfloat16)
        return carry

    lax.fori_loop(0, distinct * TILE // height, fill, 0)

    def pieces_wait(sem):
        ref = recv.at[0, pl.ds(0, workers - 1)]
        pltpu.make_async_copy(ref, ref, sem).wait()

    for chunk in range(chunks):
        pieces_wait(recv_sem.at[chunk])
        got = recv[chunk].reshape(workers * TILE, width)

        def blend(step, carry):
            result = exact_dot(
                spread[pl.ds(pl.multiple_of(step * height, height), height), :], got
            )
            mixed[chunk, pl.ds(step * (height // TILE), height // TILE)] = result.astype(
                jnp.bfloat16
            ).reshape(height // TILE, TILE, width)
            return carry

        lax.fori_loop(0, distinct * TILE // height, blend, 0)
        block = chunk * workers + me
        row = pl.multiple_of(lax.div(block, columns) * TILE, TILE)
        first = pl.multiple_of(lax.rem(block, columns) * width, 128)
        mine = (pl.ds(row, TILE), pl.ds(first, width))
        out_ref[mine] = mixed[chunk, lax.rem(me, distinct)]

        def back(step, carry):
            device = target(step)

            @pl.when(device != me)
            def _():
                pltpu.make_async_remote_copy(
                    src_ref=mixed.at[chunk, lax.rem(device, distinct)],
                    dst_ref=out_ref.at[mine],
                    send_sem=back_send_sem.at[chunk],
                    recv_sem=back_recv_sem.at[chunk],
                    device_id=coordinates(device),
                    device_id_type=MESH,
                ).start()

            return carry

        lax.fori_loop(0, workers, back, 0)

    for chunk in range(chunks):
        pieces_wait(send_sem.at[chunk])
        pieces_wait(back_send_sem.at[chunk])
        pieces_wait(back_recv_sem.at[chunk])


def shards(sizes, hidden_acts, output_grad, weights, momentum, worker_of_slot, round_shift):
    hidden = hidden_acts.reshape(hidden_acts.shape[-2:])
    grad_out = output_grad.reshape(output_grad.shape[-2:])
    weight = weights.reshape(weights.shape[-2:])
    moment = momentum.reshape(momentum.shape[-2:])
    workers = sizes[0] * sizes[1] * sizes[2]
    tokens, features = hidden.shape
    rows = weight.shape[0]
    parts = rows // TILE
    width = max(128, features // workers)
    columns = features // width
    chunks = parts * columns // workers
    distinct = workers // 2
    anywhere = pl.BlockSpec(memory_space=pl.ANY)
    vmem = pl.BlockSpec(memory_space=pltpu.VMEM)
    smem = pl.BlockSpec(memory_space=pltpu.SMEM)
    half = jnp.bfloat16
    mixed, new_moment = pl.pallas_call(
        functools.partial(kernel, sizes),
        out_shape=[jax.ShapeDtypeStruct((rows, features), half)] * 2,
        in_specs=[anywhere, vmem, anywhere, anywhere, vmem, smem],
        out_specs=[vmem, vmem],
        scratch_shapes=[
            pltpu.VMEM((columns, tokens, width), half),
            pltpu.VMEM((rows, features), half),
            pltpu.VMEM((rows, features), half),
            pltpu.VMEM((parts, columns, TILE, width), half),
            pltpu.VMEM((chunks, workers, TILE, width), half),
            pltpu.VMEM((chunks, distinct, TILE, width), half),
            pltpu.VMEM((distinct * TILE, workers * TILE), half),
            pltpu.SemaphoreType.DMA((columns,)),
            pltpu.SemaphoreType.DMA((2,)),
            pltpu.SemaphoreType.DMA((chunks,)),
            pltpu.SemaphoreType.DMA((chunks,)),
            pltpu.SemaphoreType.DMA((chunks,)),
            pltpu.SemaphoreType.DMA((chunks,)),
        ],
        compiler_params=pltpu.CompilerParams(
            collective_id=0, has_side_effects=True, vmem_limit_bytes=60 * 1024 * 1024
        ),
        name="step_and_gossip",
    )(hidden, grad_out, weight, moment, worker_of_slot.reshape(1, workers), round_shift)
    return (mixed.reshape(weights.shape), new_moment.reshape(momentum.shape))


def solution(mesh):
    sizes = (mesh.shape["gx"], mesh.shape["gy"], mesh.shape["gz"])
    placed = (
        P("gz", "gy", "gx", None, None),
        P("gz", "gy", "gx", None, None),
        P("gz", "gy", "gx", None, None),
        P("gz", "gy", "gx", None, None),
        P(),
        P(),
    )
    return jax.shard_map(
        functools.partial(shards, sizes),
        mesh=mesh,
        in_specs=placed,
        out_specs=(P("gx", "gy", "gz", None, None), P("gz", "gy", "gx", None, None)),
        check_vma=False,
    )
```

time: 83.2 us -> 62.7 us (0.75)
  Pallas kernels: 0 us -> 55.4 us
  blocking collectives: 29.6 us -> 0 us
  waiting for transfers between devices: 18.2 us -> 0 us
  matrix products: 8.11 us -> 0 us
  starting transfers between devices: 7.32 us -> 0 us
  between operations: 5.81 us -> 0.64 us
  other arithmetic: 4.95 us -> 0 us
  local copies, waits for them, and re-layouts: 8.86 us -> 5.97 us
    pallas_call x0 -> x1, Pallas kernels: none -> 55.4 us  [shards(): pl.pallas_call(functools.partial(kernel, sizes), out_shape=[jax.ShapeDtyp...]
    all_to_all x1 -> x0, blocking collectives: 29.6 us -> none  [shards(): block = lax.all_to_all(mixed, AXES, split_axis=0, concat_axis=0, tiled=True)]
    all_to_all x1 -> x0, waiting for transfers between devices: 18.2 us -> none  [shards(): got = lax.all_to_all(pieces, AXES, split_axis=0, concat_axis=0, tiled=True)]
    dot_general x2 -> x0, matrix products: 8.11 us -> none  [the longest x1 6.59 us: shards(): lax.dot_general(grad_out, hidden, (((0,), (0,)), ((), ())), preferred_ele...]
    all_to_all x1 -> x0, starting transfers between devices: 7.32 us -> none  [shards(): got = lax.all_to_all(pieces, AXES, split_axis=0, concat_axis=0, tiled=True)]
    all_to_all x2 -> x0, other arithmetic: 2.98 us -> none  [the longest x1 1.49 us: shards(): block = lax.all_to_all(mixed, AXES, split_axis=0, concat_axis=0, tiled=True)]
    reduce_sum x9 -> x0, other arithmetic: 1.82 us -> none  [the longest x8 1.43 us: mixing(): share = (share + jnp.sum(hit * share[None, :], axis=1)) * 0.5]
    unnamed x11 -> x3, local copies, waits for them, and re-layouts: 7.31 us -> 5.97 us
  transfers between devices with their start and end apart: 1 -> 0, of which waited for: 1 -> 0; matrix products, arithmetic and copies ran while one was open for 4% -> 0% of each run, Pallas kernels for 0% -> 0%
where the time goes in v2:
time: 62.7 us; the launch traced here: 62 us
  Pallas kernels  55.4 us (88%)
  local copies, waits for them, and re-layouts  5.97 us (10%)
  between operations  0.64 us (1%)
    pallas_call x1, Pallas kernels, shards(): pl.pallas_call(functools.partial(kernel, sizes), out_shape=[jax.ShapeDtyp...  55.4 us
    unnamed x3, local copies, waits for them, and re-layouts  5.97 us

profile of v2, /device:TPU:0, one launch (start us, length us, event | category | flops | bytes accessed | tf_op | source)
XLA Modules:
  0.0 62.0 jit_solution(1411442001318820029)
XLA Ops:
  0.6 1.5 %copy.8 = bf16[1,1,1,256,32]{4,3,2,1,0:T(8,128)(2,1)} copy(bf16[1,1,1,256,32]{3,4,2,1,0:T(8,128)(2,1)} %param.7) | data formatting | bytes 32768 | tf_op args[1]
  2.1 55.4 %step_and_gossip.1 = (bf16[32,16384]{1,0:T(8,128)(2,1)}, bf16[32,16384]{1,0:T(8,128)(2,1)}) custom-call(bf16[256,16384]{1,0:T(8,128)(2,1)} %bitcast.7, bf16[256,32]{1,0:T(8,128)(2,1)} %bitcast.12, bf16[32,16384]{1,0:T(8,128)(2,1)} %bitcast.10, bf16[32,16384]{1,0:T(8,128)(2,1)} %bitcast.11, s32[1,32]{1,0:T(1,128)} %bitcast.13, s32[8]{0:T(128)} %shift_ref.1), custom_call_target="tpu_custom_call" | custom-call | tf_op jit(solution)/shard_map/step_and_gossip/pallas_call | solution.py:264
  57.5 2.3 %copy.11 = bf16[1,1,1,32,16384]{4,3,2,1,0:T(8,128)(2,1)} copy(bf16[1,1,1,32,16384]{4,3,2,1,0:T(8,128)(2,1)} %bitcast.9) | data formatting | bytes 2097152
  59.8 2.3 %copy.12 = bf16[1,1,1,32,16384]{4,3,2,1,0:T(8,128)(2,1)} copy(bf16[1,1,1,32,16384]{4,3,2,1,0:T(8,128)(2,1)} %bitcast.8) | data formatting | bytes 2097152

commit v3 on v2

--- a/solution.py
+++ b/solution.py
@@ -10,6 +10,7 @@
 learn_rate = 0.01
 beta_keep = 0.9
 TILE = 16
+GROUP = 2
 MESH = pl.DeviceIdType.MESH
 
 
@@ -43,7 +44,8 @@
     mixed,
     spread,
     hidden_sem,
-    local_sem,
+    moment_sem,
+    weight_sem,
     send_sem,
     recv_sem,
     back_send_sem,
@@ -81,19 +83,22 @@
     def column(step):
         return target(step) if columns == workers else lax.rem(me + step, columns)
 
-    def load(step):
+    def loads(step):
         place = column(step)
-        return pltpu.make_async_copy(
-            hidden_hbm.at[:, pl.ds(pl.multiple_of(place * width, 128), width)],
-            hidden.at[place],
-            hidden_sem.at[step],
-        )
-
-    weight_copy = pltpu.make_async_copy(weight_hbm, weight, local_sem.at[0])
-    moment_copy = pltpu.make_async_copy(moment_hbm, moment, local_sem.at[1])
-    weight_copy.start()
-    moment_copy.start()
-    lax.fori_loop(0, columns, lambda step, c: (load(step).start(), c)[1], 0)
+        span = pl.ds(pl.multiple_of(place * width, 128), width)
+        return [
+            pltpu.make_async_copy(source.at[:, span], kept.at[place], sem.at[step])
+            for source, kept, sem in (
+                (hidden_hbm, hidden, hidden_sem),
+                (moment_hbm, moment, moment_sem),
+                (weight_hbm, weight, weight_sem),
+            )
+        ]
+
+    def load(step, carry):
+        for copy in loads(step):
+            copy.start()
+        return carry
 
     barrier = pltpu.get_barrier_semaphore()
 
@@ -109,11 +114,8 @@
         return carry
 
     lax.fori_loop(0, workers, greet, 0)
-    grad_rows = jnp.transpose(grad_ref[...].astype(jnp.float32)).astype(jnp.bfloat16)
-    weight_copy.wait()
-    moment_copy.wait()
-    pl.semaphore_wait(barrier, workers - 1)
-
+    lax.fori_loop(0, columns, load, 0)
+    grad_rows = grad_ref[...]
     def place_of(part, where):
         block = part * columns
         return block // workers, block % workers + where
@@ -135,35 +137,46 @@
     early = [part for part in range(parts) if place_of(part, 0)[0] == 0]
     late = [part for part in range(parts) if place_of(part, 0)[0] > 0]
 
-    def compute(step, carry):
-        where = column(step)
-        load(step).wait()
-        span = pl.ds(pl.multiple_of(where * width, 128), width)
-        grad = exact_dot(grad_rows, hidden[where])
-        velocity = beta_keep * moment[:, span].astype(jnp.float32) + grad
-        new_moment_ref[:, span] = velocity.astype(jnp.bfloat16)
-        stepped = (weight[:, span].astype(jnp.float32) - learn_rate * velocity).astype(
-            jnp.bfloat16
-        )
-        for part in range(parts):
-            piece = stepped[part * TILE : (part + 1) * TILE]
-            stage[part, where] = piece
-            chunk, device = place_of(part, where)
-
-            @pl.when(device == me)
-            def _():
-                recv[chunk, slot] = piece
-
-        @pl.when(step > 0)
-        def _():
+    def compute(group):
+        steps = [group * GROUP + k for k in range(GROUP)]
+        for step in steps:
+            for copy in loads(step):
+                copy.wait()
+        places = [column(step) for step in steps]
+        grads = [exact_dot(grad_rows, hidden[where]) for where in places]
+        for where, grad in zip(places, grads):
+            span = pl.ds(pl.multiple_of(where * width, 128), width)
+            velocity = beta_keep * moment[where].astype(jnp.float32) + grad
+            new_moment_ref[:, span] = velocity.astype(jnp.bfloat16)
+            stepped = (weight[where].astype(jnp.float32) - learn_rate * velocity).astype(
+                jnp.bfloat16
+            )
+            for part in range(parts):
+                piece = stepped[part * TILE : (part + 1) * TILE]
+                stage[part, where] = piece
+                chunk, device = place_of(part, where)
+
+                @pl.when(device == me)
+                def _():
+                    recv[chunk, slot] = piece
+
+    def send_early(group):
+        for k in range(GROUP):
             for part in early:
-                send(part, column(step - 1))
-
+                send(part, column(group * GROUP + k))
+
+    def compute_and_send(group, carry):
+        compute(group)
+        send_early(group - 1)
         return carry
 
-    lax.fori_loop(0, columns, compute, 0)
-    for part in early:
-        send(part, column(jnp.int32(columns - 1)))
+    groups = columns // GROUP
+    compute(jnp.int32(0))
+    pl.semaphore_wait(barrier, workers - 1)
+    send_early(jnp.int32(0))
+    compute(jnp.int32(1))
+    lax.fori_loop(2, groups, compute_and_send, 0)
+    send_early(jnp.int32(groups - 1))
     for part in late:
         lax.fori_loop(0, columns, lambda step, c: (send(part, column(step)), c)[1], 0)
 
@@ -244,9 +257,20 @@
         pieces_wait(back_recv_sem.at[chunk])
 
 
+def store(mixed_ref, moment_ref, mixed_hbm, moment_hbm, sem):
+    copies = [
+        pltpu.make_async_copy(mixed_ref, mixed_hbm, sem.at[0]),
+        pltpu.make_async_copy(moment_ref, moment_hbm, sem.at[1]),
+    ]
+    for copy in copies:
+        copy.start()
+    for copy in copies:
+        copy.wait()
+
+
 def shards(sizes, hidden_acts, output_grad, weights, momentum, worker_of_slot, round_shift):
     hidden = hidden_acts.reshape(hidden_acts.shape[-2:])
-    grad_out = output_grad.reshape(output_grad.shape[-2:])
+    grad_out = output_grad.reshape(output_grad.shape[-2:]).T
     weight = weights.reshape(weights.shape[-2:])
     moment = momentum.reshape(momentum.shape[-2:])
     workers = sizes[0] * sizes[1] * sizes[2]
@@ -263,19 +287,20 @@
     half = jnp.bfloat16
     mixed, new_moment = pl.pallas_call(
         functools.partial(kernel, sizes),
-        out_shape=[jax.ShapeDtypeStruct((rows, features), half)] * 2,
+        out_shape=[pltpu.VMEM((rows, features), half)] * 2,
         in_specs=[anywhere, vmem, anywhere, anywhere, vmem, smem],
         out_specs=[vmem, vmem],
         scratch_shapes=[
             pltpu.VMEM((columns, tokens, width), half),
-            pltpu.VMEM((rows, features), half),
-            pltpu.VMEM((rows, features), half),
+            pltpu.VMEM((columns, rows, width), half),
+            pltpu.VMEM((columns, rows, width), half),
             pltpu.VMEM((parts, columns, TILE, width), half),
             pltpu.VMEM((chunks, workers, TILE, width), half),
             pltpu.VMEM((chunks, distinct, TILE, width), half),
             pltpu.VMEM((distinct * TILE, workers * TILE), half),
             pltpu.SemaphoreType.DMA((columns,)),
-            pltpu.SemaphoreType.DMA((2,)),
+            pltpu.SemaphoreType.DMA((columns,)),
+            pltpu.SemaphoreType.DMA((columns,)),
             pltpu.SemaphoreType.DMA((chunks,)),
             pltpu.SemaphoreType.DMA((chunks,)),
             pltpu.SemaphoreType.DMA((chunks,)),
@@ -286,6 +311,17 @@
         ),
         name="step_and_gossip",
     )(hidden, grad_out, weight, moment, worker_of_slot.reshape(1, workers), round_shift)
+    mixed, new_moment = pl.pallas_call(
+        store,
+        out_shape=[jax.ShapeDtypeStruct((rows, features), half)] * 2,
+        in_specs=[anywhere, anywhere],
+        out_specs=[anywhere, anywhere],
+        scratch_shapes=[pltpu.SemaphoreType.DMA((2,))],
+        name="store",
+    )(
+        pltpu.with_memory_space_constraint(mixed, pltpu.VMEM),
+        pltpu.with_memory_space_constraint(new_moment, pltpu.VMEM),
+    )
     return (mixed.reshape(weights.shape), new_moment.reshape(momentum.shape))
 
 

time: 62.7 us -> 56.5 us (0.901)
  local copies, waits for them, and re-layouts: 5.97 us -> 0 us
    unnamed x3 -> x0, local copies, waits for them, and re-layouts: 5.97 us -> none
    pallas_call x1 -> x2, Pallas kernels: 55.4 us -> 55.2 us  [the longest x1 53.8 us: shards(): pl.pallas_call(functools.partial(kernel, sizes), out_shape=[pltpu.VMEM((r...]
where the time goes in v3:
time: 56.5 us; the launch traced here: 55.8 us
  Pallas kernels  55.2 us (98%)
  between operations  0.64 us (1%)
    pallas_call x1, Pallas kernels, shards(): pl.pallas_call(functools.partial(kernel, sizes), out_shape=[pltpu.VMEM((r...  53.8 us
    pallas_call x1, Pallas kernels, shards(): pl.pallas_call(store, out_shape=[jax.ShapeDtypeStruct((rows, features), h...  1.33 us

profile of v3, /device:TPU:0, one launch (start us, length us, event | category | flops | bytes accessed | tf_op | source)
XLA Modules:
  0.0 55.8 jit_solution(3740595102065623792)
XLA Ops:
  0.6 53.8 %step_and_gossip.1 = (bf16[32,16384]{1,0:T(8,128)(2,1)S(1)}, bf16[32,16384]{1,0:T(8,128)(2,1)S(1)}) custom-call(bf16[256,16384]{1,0:T(8,128)(2,1)} %bitcast.9, bf16[32,256]{1,0:T(8,128)(2,1)} %bitcast.12, bf16[32,16384]{1,0:T(8,128)(2,1)} %bitcast.10, bf16[32,16384]{1,0:T(8,128)(2,1)} %bitcast.11, s32[1,32]{1,0:T(1,128)} %bitcast.13, s32[8]{0:T(128)} %shift_ref.1), custom_call_target="tpu_custom_call" | custom-call | tf_op jit(solution)/shard_map/step_and_gossip/pallas_call | solution.py:288
  54.5 1.3 %store.1 = (bf16[32,16384]{1,0:T(8,128)(2,1)}, bf16[32,16384]{1,0:T(8,128)(2,1)}) custom-call(bf16[32,16384]{1,0:T(8,128)(2,1)S(1)} %get-tuple-element.6.mixed_ref, bf16[32,16384]{1,0:T(8,128)(2,1)S(1)} %get-tuple-element.7.moment_ref), custom_call_target="tpu_custom_call" | custom-call | tf_op jit(solution)/shard_map/store/pallas_call | solution.py:314

commit v4 on v3

--- a/solution.py
+++ b/solution.py
@@ -68,9 +68,9 @@
         rest = lax.rem(step, per)
         side = lax.div(my_x, half_x)
         other = far + side - 2 * far * side
+        to_y = lax.rem(my_y + lax.rem(rest, size_y), size_y)
+        to_z = lax.rem(my_z + lax.rem(lax.div(rest, size_y), size_z), size_z)
         to_x = other * half_x + lax.rem(my_x + lax.div(rest, size_y * size_z), half_x)
-        to_y = lax.rem(my_y + lax.rem(lax.div(rest, size_z), size_y), size_y)
-        to_z = lax.rem(my_z + lax.rem(rest, size_z), size_z)
         return (to_x * size_y + to_y) * size_z + to_z
 
     def coordinates(device):
@@ -233,8 +233,10 @@
         mine = (pl.ds(row, TILE), pl.ds(first, width))
         out_ref[mine] = mixed[chunk, lax.rem(me, distinct)]
 
+        turned = workers // 2 if chunk == chunks - 1 else 0
+
         def back(step, carry):
-            device = target(step)
+            device = target(lax.rem(step + turned, workers))
 
             @pl.when(device != me)
             def _():

time: 56.5 us -> 56.3 us (level)
  no operation moved by 1% of the time
where the time goes in v4:
time: 56.3 us; the launch traced here: 55.3 us
  Pallas kernels  54.7 us (97%)
  between operations  0.64 us (1%)
    pallas_call x1, Pallas kernels, shards(): pl.pallas_call(functools.partial(kernel, sizes), out_shape=[pltpu.VMEM((r...  53.4 us
    pallas_call x1, Pallas kernels, shards(): pl.pallas_call(store, out_shape=[jax.ShapeDtypeStruct((rows, features), h...  1.33 us

profile of v4, /device:TPU:0, one launch (start us, length us, event | category | flops | bytes accessed | tf_op | source)
XLA Modules:
  0.0 55.3 jit_solution(11188414653617121120)
XLA Ops:
  0.6 53.4 %step_and_gossip.1 = (bf16[32,16384]{1,0:T(8,128)(2,1)S(1)}, bf16[32,16384]{1,0:T(8,128)(2,1)S(1)}) custom-call(bf16[256,16384]{1,0:T(8,128)(2,1)} %bitcast.9, bf16[32,256]{1,0:T(8,128)(2,1)} %bitcast.12, bf16[32,16384]{1,0:T(8,128)(2,1)} %bitcast.10, bf16[32,16384]{1,0:T(8,128)(2,1)} %bitcast.11, s32[1,32]{1,0:T(1,128)} %bitcast.13, s32[8]{0:T(128)} %shift_ref.1), custom_call_target="tpu_custom_call" | custom-call | tf_op jit(solution)/shard_map/step_and_gossip/pallas_call | solution.py:290
  54.0 1.3 %store.1 = (bf16[32,16384]{1,0:T(8,128)(2,1)}, bf16[32,16384]{1,0:T(8,128)(2,1)}) custom-call(bf16[32,16384]{1,0:T(8,128)(2,1)S(1)} %get-tuple-element.6.mixed_ref, bf16[32,16384]{1,0:T(8,128)(2,1)S(1)} %get-tuple-element.7.moment_ref), custom_call_target="tpu_custom_call" | custom-call | tf_op jit(solution)/shard_map/store/pallas_call | solution.py:316
